TPU v7x, 32 devices: a whole 2x2x4 slice. The times are simulated.
32 devices in a mesh: crop: 2 (over x), seq: 2 (over y), res: 8 (over z, core).
Axes of the slice: x: 2, y: 2, z: 4, core: 2. Of those that a mesh axis runs over, the one named last changes fastest.
Arguments:
- aligned_chain_embedding: bfloat16 [128, 32, 256], P(('crop', 'seq'), 'res'), parts along dimension 0, may hold values from -6 to 6
- alignment_mask: int32 [128, 32], P(('crop', 'seq'), 'res'), parts along dimension 0, may hold values from 0 to 1, as said below
- resolved_residue_mask: int32 [64], P('crop'), parts along dimension 0, may hold values 0 or 1
- pairwise_state: bfloat16 [64, 32, 128], P(('crop', 'seq'), 'res'), parts along dimension 0, may hold values from -8 to 8
- combined_projection_matrix: bfloat16 [256, 1024], replicated, may hold values from -0.375 to 0.375
- pair_bias_weight: bfloat16 [128, 8], replicated, may hold values from -8 to 8
- final_projection_matrix: bfloat16 [256, 256], replicated, may hold values from -0.375 to 0.375
- left_right_projection_matrix: bfloat16 [256, 64], replicated, may hold values from -1.5 to 1.5
- outer_mean_weight: bfloat16 [1024, 128], replicated, may hold values from -0.1875 to 0.1875
Outputs:
- alignment_output: bfloat16 [128, 32, 256], P(('crop', 'seq'), 'res'), parts along dimension 0
- pairwise_output: bfloat16 [64, 32, 128], P(('crop', 'seq'), 'res'), parts along dimension 0
There are 2 independent parts, one for each index of `crop`. A program takes and returns all parts, laid end to end along the dimension named above; an argument that names none is the same for every part. Nothing has to cross between parts.
Inputs may be any that keep to these rules, and one draw needn't show every extreme that they name: `alignment_mask`: sequence 0 has no gaps.
All inputs are finite; a program needn't handle non-finite values.
Results may differ from a plain program's by a relative error of at most 0.013.
The roundings to bfloat16 on the way count: a program that leaves them out, or rounds other values in their place, can miss the bound.
Values may be sent and summed in bfloat16 or wider, within the bound.
A program may use at most 64 MiB of HBM per device.

v0:
```python
import math
import jax
import jax.numpy as jnp
from jax import lax
from jax.sharding import PartitionSpec as P

ROW_FEATURES = 256
CZ = 128
HEAD_NUMBER = 8
PER_HEAD_DIM = 32
PROJ_FEATURES = 32
epsilon = 1e-05


def layer_normalize(values):
    values = values.astype(jnp.float32)
    average = jnp.mean(values, axis=-1, keepdims=True)
    centered = values - average
    variance = jnp.mean(centered * centered, axis=-1, keepdims=True)
    return centered * lax.rsqrt(variance + epsilon)


def outer_rows(left_side, right_side, project):
    row_total = left_side.shape[1]
    col_total = right_side.shape[1]
    block_rows = math.gcd(row_total, max(1, 2048 // col_total))

    def outer_block(start):
        product = jnp.einsum(
            "sic,sje->ijce", left_side, right_side, preferred_element_type=jnp.float32
        )
        flattened = product.reshape(block_rows * col_total, PROJ_FEATURES * PROJ_FEATURES)
        return jnp.dot(flattened, project, precision=lax.Precision.HIGHEST).reshape(
            block_rows, col_total, CZ
        )

    starts = jnp.arange(row_total // block_rows, dtype=jnp.int32) * block_rows
    return lax.map(outer_block, starts).reshape(row_total, col_total, CZ)


def per_device(
    aligned_chain_embedding,
    alignment_mask,
    resolved_residue_mask,
    pairwise_state,
    combined_projection_matrix,
    pair_bias_weight,
    final_projection_matrix,
    left_right_projection_matrix,
    outer_mean_weight,
):
    chain_count = aligned_chain_embedding.shape[0]
    amino_count = aligned_chain_embedding.shape[1]
    res_ranks = lax.axis_size("res")
    seq_groups = lax.axis_size("seq")
    full_length = amino_count * res_ranks
    row_count = full_length // seq_groups
    item_count = HEAD_NUMBER * chain_count // res_ranks
    per_head = min(item_count, chain_count)
    head_count = item_count // per_head
    my_rank = lax.axis_index("res")
    my_group = lax.axis_index("seq")
    standardized_rows = layer_normalize(aligned_chain_embedding).astype(jnp.bfloat16)
    linear_mapped = jnp.dot(
        standardized_rows.reshape(chain_count * amino_count, ROW_FEATURES),
        combined_projection_matrix,
        preferred_element_type=jnp.float32,
    )
    linear_mapped = linear_mapped.reshape(chain_count, amino_count, 4, HEAD_NUMBER, PER_HEAD_DIM)
    queries = (linear_mapped[:, :, 0] * PER_HEAD_DIM ** (-0.5)).astype(jnp.bfloat16)
    key_rows = linear_mapped[:, :, 1].astype(jnp.bfloat16)
    value_rows = linear_mapped[:, :, 2].astype(jnp.bfloat16)
    sigmoid_factor = jax.nn.sigmoid(linear_mapped[:, :, 3])
    stacked = jnp.stack([queries, key_rows, value_rows], axis=2)
    stacked = jnp.transpose(stacked, (3, 0, 1, 2, 4)).reshape(
        HEAD_NUMBER * chain_count, amino_count, 3 * PER_HEAD_DIM
    )
    presence_mask_flags = alignment_mask.astype(jnp.bfloat16)
    key_flags = jnp.broadcast_to(
        presence_mask_flags[None], (HEAD_NUMBER, chain_count, amino_count)
    ).reshape(HEAD_NUMBER * chain_count, amino_count)
    arrived, arrived_flags = (
        lax.all_to_all(stacked, "res", split_axis=0, concat_axis=1, tiled=True),
        lax.all_to_all(key_flags, "res", split_axis=0, concat_axis=1, tiled=True),
    )
    pair_normed = layer_normalize(pairwise_state).astype(jnp.bfloat16)
    local_bias = jnp.dot(
        pair_normed.reshape(row_count * amino_count, CZ),
        pair_bias_weight,
        preferred_element_type=jnp.float32,
    )
    local_bias = jnp.transpose(
        local_bias.astype(jnp.bfloat16).reshape(row_count, amino_count, HEAD_NUMBER), (2, 0, 1)
    )
    bias_cols = lax.all_gather(local_bias, "res", axis=2, tiled=True)
    whole_bias = lax.all_gather(bias_cols, "seq", axis=1, tiled=True)
    first_head = my_rank * item_count // chain_count
    head_bias = lax.dynamic_slice_in_dim(whole_bias, first_head, head_count, 0)
    grouped = arrived.reshape(head_count, per_head, full_length, 3, PER_HEAD_DIM)
    key_validity_mask = (
        arrived_flags.reshape(head_count, per_head, full_length).astype(jnp.float32) - 1.0
    ) * 1000000000.0
    scores = jnp.einsum(
        "gpid,gpjd->gpij",
        grouped[:, :, :, 0],
        grouped[:, :, :, 1],
        preferred_element_type=jnp.float32,
    )
    scores = scores + head_bias.astype(jnp.float32)[:, None] + key_validity_mask[:, :, None, :]
    row_max = jnp.max(scores, axis=-1, keepdims=True)
    exponent = jnp.exp(scores - row_max)
    weights = (exponent / jnp.sum(exponent, axis=-1, keepdims=True)).astype(jnp.bfloat16)
    softmax_mixed = jnp.einsum(
        "gpij,gpjd->gpid", weights, grouped[:, :, :, 2], preferred_element_type=jnp.float32
    )
    softmax_mixed = softmax_mixed.astype(jnp.bfloat16).reshape(
        item_count, full_length, PER_HEAD_DIM
    )
    returned = lax.all_to_all(softmax_mixed, "res", split_axis=1, concat_axis=0, tiled=True)
    returned = jnp.transpose(
        returned.reshape(HEAD_NUMBER, chain_count, amino_count, PER_HEAD_DIM), (1, 2, 0, 3)
    )
    sigmoid_scaled = (
        (sigmoid_factor * returned.astype(jnp.float32))
        .astype(jnp.bfloat16)
        .reshape(chain_count * amino_count, ROW_FEATURES)
    )
    embedding_increment = jnp.dot(
        sigmoid_scaled, final_projection_matrix, preferred_element_type=jnp.float32
    ).reshape(chain_count, amino_count, ROW_FEATURES)
    alignment_output = (aligned_chain_embedding.astype(jnp.float32) + embedding_increment).astype(
        jnp.bfloat16
    )
    standardized_product = layer_normalize(alignment_output).astype(jnp.bfloat16)
    left_right_vectors = jnp.dot(
        standardized_product.reshape(chain_count * amino_count, ROW_FEATURES),
        left_right_projection_matrix,
        preferred_element_type=jnp.float32,
    )
    left_right_vectors = left_right_vectors.reshape(chain_count, amino_count, 2, PROJ_FEATURES)
    entry_present = alignment_mask.astype(jnp.float32)[:, :, None]
    left_side = (left_right_vectors[:, :, 0] * entry_present).astype(jnp.bfloat16)
    right_side = (left_right_vectors[:, :, 1] * entry_present).astype(jnp.bfloat16)
    left_all, left_flags = (
        lax.all_gather(left_side, "res", axis=1, tiled=True),
        lax.all_gather(presence_mask_flags, "res", axis=1, tiled=True),
    )
    project = outer_mean_weight.astype(jnp.float32)
    row_start = my_group * row_count
    left_full, flag_full = (
        lax.all_to_all(left_all, "seq", split_axis=1, concat_axis=0, tiled=True),
        lax.all_to_all(left_flags, "seq", split_axis=1, concat_axis=0, tiled=True),
    )
    right_full, right_flags = (
        lax.all_gather(right_side, "seq", axis=0, tiled=True),
        lax.all_gather(presence_mask_flags, "seq", axis=0, tiled=True),
    )
    counts = jnp.dot(flag_full.T, right_flags, preferred_element_type=jnp.float32)
    outer = outer_rows(left_full, right_full, project)
    col_start = my_rank * amino_count
    row_mask = lax.dynamic_slice_in_dim(resolved_residue_mask, row_start, row_count).astype(
        jnp.float32
    )
    col_mask = lax.dynamic_slice_in_dim(resolved_residue_mask, col_start, amino_count).astype(
        jnp.float32
    )
    pair_mask = row_mask[:, None] * col_mask[None, :]
    pairwise_output = (
        pairwise_state.astype(jnp.float32) + pair_mask[:, :, None] * (outer / counts[:, :, None])
    ).astype(jnp.bfloat16)
    return (alignment_output, pairwise_output)


def solution(mesh):
    placed = (
        P(("crop", "seq"), "res", None),
        P(("crop", "seq"), "res"),
        P("crop"),
        P(("crop", "seq"), "res", None),
        P(),
        P(),
        P(),
        P(),
        P(),
    )
    return jax.shard_map(
        per_device,
        mesh=mesh,
        in_specs=placed,
        out_specs=(P(("crop", "seq"), "res", None), P(("crop", "seq"), "res", None)),
        check_vma=False,
    )
```

profile of v0, /device:TPU:0, one launch (start us, length us, event | category | flops | bytes accessed | tf_op | source)
XLA Modules:
  0.0 115.8 jit_solution(7931450124926292603)
XLA Ops:
  1.4 13.5 %all-gather = bf16[8,4,32]{2,1,0:T(4,128)(2,1)S(1)} all-gather(bf16[1,4,32]{2,1,0:T(4,128)(2,1)S(1)} %bitcast.150), channel_id=1, replica_groups=mesh['crop'=2,'seq'=2,'res'=8] {'res'}, dimensions={0}, use_global_device_ids=true | all-gather | bytes 2304 | tf_op jit(solution)/shard_map/all_gather | solution.py:146
  15.5 3.2 %all-to-all-start.4 = ((bf16[2,2,256]{2,1,0:T(2,128)(2,1)}), bf16[2,2,256]{2,1,0:T(2,128)(2,1)S(1)}, u32[]{:S(2)}, u32[]{:S(2)}) async-start(bf16[2,2,256]{2,1,0:T(2,128)(2,1)} %reshape.211), calls=%async_computation.4 | async-start | bytes 4096 | tf_op jit(solution)/shard_map/all_to_all | solution.py:152
  18.8 1.2 %copy.71 = bf16[256,1024]{0,1:T(8,128)(2,1)S(1)} copy(bf16[256,1024]{1,0:T(8,128)(2,1)} %param.13) | data formatting | bytes 1048576 | tf_op args[4]
  20.0 0.9 convert_reduce_fusion
  21.0 1.0 fusion.21
  22.0 1.4 %fusion.30 = f32[32,4,4,8,32]{4,0,3,2,1:T(8,128)S(1)} fusion(bf16[4,8,32,256,1]{3,2,1,0,4:T(8,128)(2,1)S(1)} %bitcast.138, f32[32,4]{0,1:T(4,128)S(1)} %add_rsqrt_fusion.2, f32[32,4]{0,1:T(4,128)S(1)} %broadcast_multiply_fusion.3, bf16[32,4,256]{2,1,0:T(4,128)(2,1)} %param.9), kind=kOutput, calls=%fused_computation.47 | convolution fusion | flops 67239936 | bytes 1115136 | tf_op jit(solution)/shard_map/dot_general | solution.py:64
  24.3 14.0 %all_gather.18 = bf16[8,16,32]{1,0,2:T(8,128)(2,1)S(1)} all-gather(bf16[8,16,4]{1,0,2:T(8,128)(2,1)S(1)} %copy.81), channel_id=1, replica_groups=mesh['crop'=2,'seq'=2,'res'=8] {'res'}, dimensions={2}, use_global_device_ids=true | all-gather | bytes 9216 | tf_op jit(solution)/shard_map/all_gather | solution.py:95
  38.5 4.6 %all_gather.19 = bf16[8,32,32]{2,0,1:T(8,128)(2,1)S(1)} all-gather(bf16[8,16,32]{2,0,1:T(8,128)(2,1)S(1)} %copy.82), channel_id=1, replica_groups=mesh['crop'=2,'seq'=2,'res'=8] {'seq'}, dimensions={1}, use_global_device_ids=true | all-gather | bytes 24576 | tf_op jit(solution)/shard_map/all_gather | solution.py:96
  43.1 1.0 maximum_bitcast_fusion
  44.8 3.3 %all-to-all-start.1 = ((bf16[8,32,4]{1,2,0:T(4,128)(2,1)}), bf16[8,32,4]{1,2,0:T(4,128)(2,1)S(1)}, u32[]{:S(2)}, u32[]{:S(2)}) async-start(bf16[8,32,4]{1,2,0:T(4,128)(2,1)} %broadcast_in_dim.4), calls=%async_computation.1 | async-start | bytes 16384 | tf_op jit(solution)/shard_map/all_to_all | solution.py:84
  48.2 1.8 %copy.103 = bf16[8,32,4,3,32]{4,3,2,1,0:T(4,128)(2,1)S(1)} copy(bf16[8,32,4,3,32]{4,1,0,3,2:T(8,128)(2,1)} %maximum_bitcast_fusion) | data formatting | bytes 393216 | tf_op jit(solution)/shard_map/reshape | solution.py:75
  50.0 1.2 %reshape.205 = bf16[256,4,96]{2,1,0:T(4,128)(2,1)} reshape(bf16[8,32,4,3,32]{4,3,2,1,0:T(4,128)(2,1)S(1)} %copy.103) | data formatting | bytes 393216 | tf_op jit(solution)/shard_map/reshape | solution.py:75
  51.3 4.2 %all-gather.1 = bf16[2,32,4]{1,2,0:T(4,128)(2,1)S(1)} all-gather(bf16[1,32,4]{1,2,0:T(4,128)(2,1)S(1)} %bitcast.151), channel_id=1, replica_groups=mesh['crop'=2,'seq'=2,'res'=8] {'seq'}, dimensions={0}, use_global_device_ids=true | all-gather | bytes 768 | tf_op jit(solution)/shard_map/all_gather | solution.py:156
  55.6 5.0 %all-to-all-start = ((bf16[256,4,96]{2,1,0:T(4,128)(2,1)}), bf16[256,4,96]{2,1,0:T(4,128)(2,1)S(1)}, u32[]{:S(2)}, u32[]{:S(2)}) async-start(bf16[256,4,96]{2,1,0:T(4,128)(2,1)} %reshape.205), calls=%async_computation | async-start | bytes 524288 | tf_op jit(solution)/shard_map/all_to_all | solution.py:83
  60.9 9.5 %all-to-all-done = bf16[256,4,96]{2,1,0:T(4,128)(2,1)S(1)} async-done(((bf16[256,4,96]{2,1,0:T(4,128)(2,1)}), bf16[256,4,96]{2,1,0:T(4,128)(2,1)S(1)}, u32[]{:S(2)}, u32[]{:S(2)}) %all-to-all-start) | async-done | bytes 196640 | tf_op jit(solution)/shard_map/all_to_all | solution.py:83
  71.1 2.2 %reshape.185 = bf16[1,32,32,3,32]{4,3,1,2,0:T(4,128)(2,1)S(1)} reshape(bf16[32,8,4,96]{3,0,2,1:T(8,128)(2,1)} %copy.75) | data formatting | bytes 393216 | tf_op jit(solution)/shard_map/reshape | solution.py:99
  73.3 2.0 %fusion.48 = (bf16[1,32,32,1,32]{4,3,1,2,0:T(2,128)(2,1)S(1)}, bf16[1,32,32,1,32]{4,3,1,2,0:T(2,128)(2,1)S(1)}, bf16[1,32,32,1,32]{4,3,1,2,0:T(2,128)(2,1)}) fusion(bf16[1,32,32,3,32]{4,3,1,2,0:T(4,128)(2,1)S(1)} %reshape.185), kind=kLoop, calls=%fused_computation.80 | loop fusion | bytes 393216 | tf_op jit(solution)/shard_map/slice | solution.py:105
  76.2 1.5 %convolution_convert_fusion = bf16[32,32,32]{2,1,0:T(8,128)(2,1)S(1)} fusion(bf16[1,32,32,1,32]{4,3,1,2,0:T(2,128)(2,1)} %get-tuple-element.27, f32[32,32]{1,0:T(8,128)S(1)} %fusion.50, f32[32,32,32]{1,2,0:T(8,128)S(1)} %fusion.3), kind=kOutput, calls=%fused_computation.6 | convolution fusion | flops 2229279 | bytes 266240 | tf_op jit(solution)/shard_map/gpij,gpjd->gpid/dot_general | solution.py:113
  77.9 0.9 reshape.207
  78.8 3.4 %all-to-all-start.2 = ((bf16[8,2,2048]{2,1,0:T(2,128)(2,1)}), bf16[8,2,2048]{2,1,0:T(2,128)(2,1)S(1)}, u32[]{:S(2)}, u32[]{:S(2)}) async-start(bf16[8,2,2048]{2,1,0:T(2,128)(2,1)} %reshape.207), calls=%async_computation.2 | async-start | bytes 131072 | tf_op jit(solution)/shard_map/all_to_all | solution.py:119
  82.2 5.7 %all-to-all-done.2 = bf16[8,2,2048]{2,1,0:T(2,128)(2,1)S(1)} async-done(((bf16[8,2,2048]{2,1,0:T(2,128)(2,1)}), bf16[8,2,2048]{2,1,0:T(2,128)(2,1)S(1)}, u32[]{:S(2)}, u32[]{:S(2)}) %all-to-all-start.2) | async-done | bytes 65568 | tf_op jit(solution)/shard_map/all_to_all | solution.py:119
  89.4 14.2 %all_gather.21 = bf16[32,32,32]{2,0,1:T(8,128)(2,1)S(1)} all-gather(bf16[32,4,32]{2,0,1:T(8,128)(2,1)S(1)} %get-tuple-element.29), channel_id=1, replica_groups=mesh['crop'=2,'seq'=2,'res'=8] {'res'}, dimensions={1}, use_global_device_ids=true | all-gather | bytes 73728 | tf_op jit(solution)/shard_map/all_gather | solution.py:145
  104.5 3.3 %all-to-all-start.3 = ((bf16[2,2,8192]{2,1,0:T(2,128)(2,1)}), bf16[2,2,8192]{2,1,0:T(2,128)(2,1)S(1)}, u32[]{:S(2)}, u32[]{:S(2)}) async-start(bf16[2,2,8192]{2,1,0:T(2,128)(2,1)} %reshape.209), calls=%async_computation.3 | async-start | bytes 131072 | tf_op jit(solution)/shard_map/all_to_all | solution.py:151
  108.6 4.6 %all_gather.20 = bf16[64,4,32]{2,0,1:T(8,128)(2,1)S(1)} all-gather(bf16[32,4,32]{2,0,1:T(8,128)(2,1)S(1)} %get-tuple-element.28), channel_id=1, replica_groups=mesh['crop'=2,'seq'=2,'res'=8] {'seq'}, dimensions={0}, use_global_device_ids=true | all-gather | bytes 24576 | tf_op jit(solution)/shard_map/all_gather | solution.py:155
  (74 shorter events, 11.0 us)
Async XLA Ops:
  0.6 114.3 %copy-start = (bf16[1024,128]{1,0:T(8,128)(2,1)S(1)}, bf16[1024,128]{1,0:T(8,128)(2,1)}, u32[]{:S(2)}) copy-start(bf16[1024,128]{1,0:T(8,128)(2,1)} %param.17) | copy-start | bytes 786436
  15.5 28.7 %all-to-all-start.4 = ((bf16[2,2,256]{2,1,0:T(2,128)(2,1)}), bf16[2,2,256]{2,1,0:T(2,128)(2,1)S(1)}, u32[]{:S(2)}, u32[]{:S(2)}) async-start(bf16[2,2,256]{2,1,0:T(2,128)(2,1)} %reshape.211), calls=%async_computation.4 | async-start | bytes 4096 | tf_op jit(solution)/shard_map/all_to_all | solution.py:152
  22.0 1.6 %copy-start.2 = (bf16[16,4,128]{2,1,0:T(4,128)(2,1)S(1)}, bf16[16,4,128]{2,1,0:T(4,128)(2,1)}, u32[]{:S(2)}) copy-start(bf16[16,4,128]{2,1,0:T(4,128)(2,1)} %param.12) | copy-start | bytes 49156
  22.0 2.0 %copy-start.5 = (bf16[128,8]{0,1:T(8,128)(2,1)S(1)}, bf16[128,8]{0,1:T(8,128)(2,1)}, u32[]{:S(2)}) copy-start(bf16[128,8]{0,1:T(8,128)(2,1)} %param.14) | copy-start | bytes 6148
  23.4 20.7 %copy-start.6 = (s32[32]{0:T(128)S(1)}, s32[32]{0:T(128)}, u32[]{:S(2)}) copy-start(s32[32]{0:T(128)} %param.11) | copy-start | bytes 388
  44.8 10.8 %all-to-all-start.1 = ((bf16[8,32,4]{1,2,0:T(4,128)(2,1)}), bf16[8,32,4]{1,2,0:T(4,128)(2,1)S(1)}, u32[]{:S(2)}, u32[]{:S(2)}) async-start(bf16[8,32,4]{1,2,0:T(4,128)(2,1)} %broadcast_in_dim.4), calls=%async_computation.1 | async-start | bytes 16384 | tf_op jit(solution)/shard_map/all_to_all | solution.py:84
  55.6 14.7 %all-to-all-start = ((bf16[256,4,96]{2,1,0:T(4,128)(2,1)}), bf16[256,4,96]{2,1,0:T(4,128)(2,1)S(1)}, u32[]{:S(2)}, u32[]{:S(2)}) async-start(bf16[256,4,96]{2,1,0:T(4,128)(2,1)} %reshape.205), calls=%async_computation | async-start | bytes 524288 | tf_op jit(solution)/shard_map/all_to_all | solution.py:83
  77.7 10.9 %copy-start.1 = (bf16[32,4,256]{2,1,0:T(4,128)(2,1)S(1)}, bf16[32,4,256]{2,1,0:T(4,128)(2,1)}, u32[]{:S(2)}) copy-start(bf16[32,4,256]{2,1,0:T(4,128)(2,1)} %param.9) | copy-start | bytes 196612
  77.7 10.9 %copy-start.3 = (bf16[256,256]{1,0:T(8,128)(2,1)S(1)}, bf16[256,256]{1,0:T(8,128)(2,1)}, u32[]{:S(2)}) copy-start(bf16[256,256]{1,0:T(8,128)(2,1)} %param.15) | copy-start | bytes 393220
  77.7 11.4 %copy-start.4 = (bf16[256,64]{0,1:T(8,128)(2,1)S(1)}, bf16[256,64]{0,1:T(8,128)(2,1)}, u32[]{:S(2)}) copy-start(bf16[256,64]{0,1:T(8,128)(2,1)} %param.16) | copy-start | bytes 98308
  78.8 9.2 %all-to-all-start.2 = ((bf16[8,2,2048]{2,1,0:T(2,128)(2,1)}), bf16[8,2,2048]{2,1,0:T(2,128)(2,1)S(1)}, u32[]{:S(2)}, u32[]{:S(2)}) async-start(bf16[8,2,2048]{2,1,0:T(2,128)(2,1)} %reshape.207), calls=%async_computation.2 | async-start | bytes 131072 | tf_op jit(solution)/shard_map/all_to_all | solution.py:119
  104.5 8.7 %all-to-all-start.3 = ((bf16[2,2,8192]{2,1,0:T(2,128)(2,1)}), bf16[2,2,8192]{2,1,0:T(2,128)(2,1)S(1)}, u32[]{:S(2)}, u32[]{:S(2)}) async-start(bf16[2,2,8192]{2,1,0:T(2,128)(2,1)} %reshape.209), calls=%async_computation.3 | async-start | bytes 131072 | tf_op jit(solution)/shard_map/all_to_all | solution.py:151
where the time goes:
time: 117 us; the launch traced here: 116 us
  blocking collectives  55 us (47%)
  starting transfers between devices  18.2 us (16%)
  local copies, waits for them, and re-layouts  16.4 us (14%)
  waiting for transfers between devices  15.2 us (13%)
  matrix products  4.99 us (4%)
  other arithmetic  4.97 us (4%)
    all_gather x1, blocking collectives, per_device(): lax.all_gather(left_side, 'res', axis=1, tiled=True)  14.2 us
    all_gather x1, blocking collectives, per_device(): bias_cols = lax.all_gather(local_bias, 'res', axis=2, tiled=True)  14 us
    all_gather x1, blocking collectives, per_device(): lax.all_gather(presence_mask_flags, 'res', axis=1, tiled=True)  13.5 us
    all_to_all x1, waiting for transfers between devices, per_device(): lax.all_to_all(stacked, 'res', split_axis=0, concat_axis=1, tiled=True)  9.47 us
    all_to_all x1, waiting for transfers between devices, per_device(): lax.all_to_all(softmax_mixed, 'res', split_axis=1, concat_axis=0, tiled=T...  5.73 us
    unnamed x24, local copies, waits for them, and re-layouts  5.6 us
    all_to_all x1, starting transfers between devices, per_device(): lax.all_to_all(stacked, 'res', split_axis=0, concat_axis=1, tiled=True)  5.02 us
    all_gather x1, blocking collectives, per_device(): whole_bias = lax.all_gather(bias_cols, 'seq', axis=1, tiled=True)  4.58 us
  transfers between devices with their start and end apart: 5, of which 2 were waited for; matrix products, arithmetic and copies ran while one was open for 9% of the time, Pallas kernels for 0%

commit v1 on v0

--- a/solution.py
+++ b/solution.py
@@ -142,7 +142,7 @@
     left_side = (left_right_vectors[:, :, 0] * entry_present).astype(jnp.bfloat16)
     right_side = (left_right_vectors[:, :, 1] * entry_present).astype(jnp.bfloat16)
     left_all, left_flags = (
-        lax.all_gather(left_side, "res", axis=1, tiled=True),
+        jnp.concatenate(lax.all_gather(left_side, "res"), axis=1),
         lax.all_gather(presence_mask_flags, "res", axis=1, tiled=True),
     )
     project = outer_mean_weight.astype(jnp.float32)

time: 117 us -> 115 us (0.983)
  local copies, waits for them, and re-layouts: 16.4 us -> 15.2 us
  transfers between devices with their start and end apart: 5 -> 5, of which waited for: 2 -> 2; matrix products, arithmetic and copies ran while one was open for 9% -> 8% of each run, Pallas kernels for 0% -> 0%
where the time goes in v1:
time: 115 us; the launch traced here: 114 us
  blocking collectives  55.1 us (48%)
  starting transfers between devices  18.2 us (16%)
  waiting for transfers between devices  15.3 us (13%)
  local copies, waits for them, and re-layouts  15.2 us (13%)
  matrix products  4.97 us (4%)
  other arithmetic  4.18 us (4%)
    all_gather x1, blocking collectives, per_device(): lax.all_gather(left_side, 'res')  14.2 us
    all_gather x1, blocking collectives, per_device(): bias_cols = lax.all_gather(local_bias, 'res', axis=2, tiled=True)  14 us
    all_gather x1, blocking collectives, per_device(): lax.all_gather(presence_mask_flags, 'res', axis=1, tiled=True)  13.5 us
    all_to_all x1, waiting for transfers between devices, per_device(): lax.all_to_all(stacked, 'res', split_axis=0, concat_axis=1, tiled=True)  9.52 us
    all_to_all x1, waiting for transfers between devices, per_device(): lax.all_to_all(softmax_mixed, 'res', split_axis=1, concat_axis=0, tiled=T...  5.73 us
    unnamed x24, local copies, waits for them, and re-layouts  5.61 us
    all_to_all x1, starting transfers between devices, per_device(): lax.all_to_all(stacked, 'res', split_axis=0, concat_axis=1, tiled=True)  5.03 us
    all_gather x1, blocking collectives, per_device(): whole_bias = lax.all_gather(bias_cols, 'seq', axis=1, tiled=True)  4.58 us
  transfers between devices with their start and end apart: 5, of which 2 were waited for; matrix products, arithmetic and copies ran while one was open for 8% of the time, Pallas kernels for 0%

profile of v1, /device:TPU:0, one launch (start us, length us, event | category | flops | bytes accessed | tf_op | source)
XLA Modules:
  0.0 114.0 jit_solution(12454419415420637431)
XLA Ops:
  0.6 0.8 fusion.49
  1.4 13.5 %all-gather = bf16[8,4,32]{2,1,0:T(4,128)(2,1)S(1)} all-gather(bf16[1,4,32]{2,1,0:T(4,128)(2,1)S(1)} %bitcast.151), channel_id=1, replica_groups=mesh['crop'=2,'seq'=2,'res'=8] {'res'}, dimensions={0}, use_global_device_ids=true | all-gather | bytes 2304 | tf_op jit(solution)/shard_map/all_gather | solution.py:146
  15.5 3.2 %all-to-all-start.4 = ((bf16[2,2,256]{2,1,0:T(2,128)(2,1)}), bf16[2,2,256]{2,1,0:T(2,128)(2,1)S(1)}, u32[]{:S(2)}, u32[]{:S(2)}) async-start(bf16[2,2,256]{2,1,0:T(2,128)(2,1)} %reshape.232), calls=%async_computation.4 | async-start | bytes 4096 | tf_op jit(solution)/shard_map/all_to_all | solution.py:152
  18.8 1.2 %copy.124 = bf16[256,1024]{0,1:T(8,128)(2,1)S(1)} copy(bf16[256,1024]{1,0:T(8,128)(2,1)} %param.13) | data formatting | bytes 1048576 | tf_op args[4]
  20.1 0.9 convert_reduce_fusion
  21.0 1.0 fusion.21
  22.0 1.4 %fusion.30 = f32[32,4,4,8,32]{4,0,3,2,1:T(8,128)S(1)} fusion(bf16[4,8,32,256,1]{3,2,1,0,4:T(8,128)(2,1)S(1)} %bitcast.140, f32[32,4]{0,1:T(4,128)S(1)} %add_rsqrt_fusion.2, f32[32,4]{0,1:T(4,128)S(1)} %broadcast_multiply_fusion.3, bf16[32,4,256]{2,1,0:T(4,128)(2,1)} %param.9), kind=kOutput, calls=%fused_computation.47 | convolution fusion | flops 67239936 | bytes 1115136 | tf_op jit(solution)/shard_map/dot_general | solution.py:64
  24.3 14.0 %all_gather.19 = bf16[8,16,32]{1,0,2:T(8,128)(2,1)S(1)} all-gather(bf16[8,16,4]{1,0,2:T(8,128)(2,1)S(1)} %copy.134), channel_id=1, replica_groups=mesh['crop'=2,'seq'=2,'res'=8] {'res'}, dimensions={2}, use_global_device_ids=true | all-gather | bytes 9216 | tf_op jit(solution)/shard_map/all_gather | solution.py:95
  38.4 4.6 %all_gather.20 = bf16[8,32,32]{2,0,1:T(8,128)(2,1)S(1)} all-gather(bf16[8,16,32]{2,0,1:T(8,128)(2,1)S(1)} %copy.135), channel_id=1, replica_groups=mesh['crop'=2,'seq'=2,'res'=8] {'seq'}, dimensions={1}, use_global_device_ids=true | all-gather | bytes 24576 | tf_op jit(solution)/shard_map/all_gather | solution.py:96
  43.9 3.3 %all-to-all-start.1 = ((bf16[8,32,4]{1,2,0:T(4,128)(2,1)}), bf16[8,32,4]{1,2,0:T(4,128)(2,1)S(1)}, u32[]{:S(2)}, u32[]{:S(2)}) async-start(bf16[8,32,4]{1,2,0:T(4,128)(2,1)} %broadcast_in_dim.4), calls=%async_computation.1 | async-start | bytes 16384 | tf_op jit(solution)/shard_map/all_to_all | solution.py:84
  48.1 1.2 %reshape.226 = bf16[256,4,96]{2,1,0:T(4,128)(2,1)} reshape(bf16[8,32,4,3,32]{4,3,2,1,0:T(4,128)(2,1)S(1)} %copy.156) | data formatting | bytes 393216 | tf_op jit(solution)/shard_map/reshape | solution.py:75
  49.4 4.2 %all-gather.1 = bf16[2,32,4]{1,2,0:T(4,128)(2,1)S(1)} all-gather(bf16[1,32,4]{1,2,0:T(4,128)(2,1)S(1)} %bitcast.152), channel_id=1, replica_groups=mesh['crop'=2,'seq'=2,'res'=8] {'seq'}, dimensions={0}, use_global_device_ids=true | all-gather | bytes 768 | tf_op jit(solution)/shard_map/all_gather | solution.py:156
  53.8 5.0 %all-to-all-start = ((bf16[256,4,96]{2,1,0:T(4,128)(2,1)}), bf16[256,4,96]{2,1,0:T(4,128)(2,1)S(1)}, u32[]{:S(2)}, u32[]{:S(2)}) async-start(bf16[256,4,96]{2,1,0:T(4,128)(2,1)} %reshape.226), calls=%async_computation | async-start | bytes 524288 | tf_op jit(solution)/shard_map/all_to_all | solution.py:83
  59.0 9.5 %all-to-all-done = bf16[256,4,96]{2,1,0:T(4,128)(2,1)S(1)} async-done(((bf16[256,4,96]{2,1,0:T(4,128)(2,1)}), bf16[256,4,96]{2,1,0:T(4,128)(2,1)S(1)}, u32[]{:S(2)}, u32[]{:S(2)}) %all-to-all-start) | async-done | bytes 196640 | tf_op jit(solution)/shard_map/all_to_all | solution.py:83
  69.3 2.2 %reshape.204 = bf16[1,32,32,3,32]{4,3,1,2,0:T(4,128)(2,1)S(1)} reshape(bf16[32,8,4,96]{3,0,2,1:T(8,128)(2,1)} %copy.128) | data formatting | bytes 393216 | tf_op jit(solution)/shard_map/reshape | solution.py:99
  71.5 2.0 %fusion.48 = (bf16[1,32,32,1,32]{4,3,1,2,0:T(2,128)(2,1)S(1)}, bf16[1,32,32,1,32]{4,3,1,2,0:T(2,128)(2,1)S(1)}, bf16[1,32,32,1,32]{4,3,1,2,0:T(2,128)(2,1)}) fusion(bf16[1,32,32,3,32]{4,3,1,2,0:T(4,128)(2,1)S(1)} %reshape.204), kind=kLoop, calls=%fused_computation.80 | loop fusion | bytes 393216 | tf_op jit(solution)/shard_map/slice | solution.py:105
  74.3 1.5 %convolution_convert_fusion = bf16[32,32,32]{2,1,0:T(8,128)(2,1)S(1)} fusion(bf16[1,32,32,1,32]{4,3,1,2,0:T(2,128)(2,1)} %get-tuple-element.31, f32[32,32]{1,0:T(8,128)S(1)} %fusion.50, f32[32,32,32]{1,2,0:T(8,128)S(1)} %fusion.3), kind=kOutput, calls=%fused_computation.6 | convolution fusion | flops 2229279 | bytes 266240 | tf_op jit(solution)/shard_map/gpij,gpjd->gpid/dot_general | solution.py:113
  76.0 0.9 reshape.228
  77.0 3.4 %all-to-all-start.2 = ((bf16[8,2,2048]{2,1,0:T(2,128)(2,1)}), bf16[8,2,2048]{2,1,0:T(2,128)(2,1)S(1)}, u32[]{:S(2)}, u32[]{:S(2)}) async-start(bf16[8,2,2048]{2,1,0:T(2,128)(2,1)} %reshape.228), calls=%async_computation.2 | async-start | bytes 131072 | tf_op jit(solution)/shard_map/all_to_all | solution.py:119
  80.4 5.7 %all-to-all-done.2 = bf16[8,2,2048]{2,1,0:T(2,128)(2,1)S(1)} async-done(((bf16[8,2,2048]{2,1,0:T(2,128)(2,1)}), bf16[8,2,2048]{2,1,0:T(2,128)(2,1)S(1)}, u32[]{:S(2)}, u32[]{:S(2)}) %all-to-all-start.2) | async-done | bytes 65568 | tf_op jit(solution)/shard_map/all_to_all | solution.py:119
  87.6 14.2 %all_gather.22 = bf16[8,32,4,32]{3,1,2,0:T(8,128)(2,1)S(1)} all-gather(bf16[1,32,4,32]{3,1,2,0:T(8,128)(2,1)S(1)} %fusion.33), channel_id=1, replica_groups=mesh['crop'=2,'seq'=2,'res'=8] {'res'}, dimensions={0}, use_global_device_ids=true | all-gather | bytes 73728 | tf_op jit(solution)/shard_map/all_gather | solution.py:145
  101.8 0.9 reshape.230
  102.7 3.3 %all-to-all-start.3 = ((bf16[2,2,8192]{2,1,0:T(2,128)(2,1)}), bf16[2,2,8192]{2,1,0:T(2,128)(2,1)S(1)}, u32[]{:S(2)}, u32[]{:S(2)}) async-start(bf16[2,2,8192]{2,1,0:T(2,128)(2,1)} %reshape.230), calls=%async_computation.3 | async-start | bytes 131072 | tf_op jit(solution)/shard_map/all_to_all | solution.py:151
  106.8 4.6 %all_gather.21 = bf16[64,4,32]{2,0,1:T(8,128)(2,1)S(1)} all-gather(bf16[32,4,32]{2,0,1:T(8,128)(2,1)S(1)} %fusion.35), channel_id=1, replica_groups=mesh['crop'=2,'seq'=2,'res'=8] {'seq'}, dimensions={0}, use_global_device_ids=true | all-gather | bytes 24576 | tf_op jit(solution)/shard_map/all_gather | solution.py:155
  (75 shorter events, 10.3 us)
Async XLA Ops:
  0.6 112.5 %copy-start = (bf16[1024,128]{1,0:T(8,128)(2,1)S(1)}, bf16[1024,128]{1,0:T(8,128)(2,1)}, u32[]{:S(2)}) copy-start(bf16[1024,128]{1,0:T(8,128)(2,1)} %param.17) | copy-start | bytes 786436
  15.5 27.8 %all-to-all-start.4 = ((bf16[2,2,256]{2,1,0:T(2,128)(2,1)}), bf16[2,2,256]{2,1,0:T(2,128)(2,1)S(1)}, u32[]{:S(2)}, u32[]{:S(2)}) async-start(bf16[2,2,256]{2,1,0:T(2,128)(2,1)} %reshape.232), calls=%async_computation.4 | async-start | bytes 4096 | tf_op jit(solution)/shard_map/all_to_all | solution.py:152
  18.8 4.8 %copy-start.2 = (bf16[16,4,128]{2,1,0:T(4,128)(2,1)S(1)}, bf16[16,4,128]{2,1,0:T(4,128)(2,1)}, u32[]{:S(2)}) copy-start(bf16[16,4,128]{2,1,0:T(4,128)(2,1)} %param.12) | copy-start | bytes 49156
  20.0 3.9 %copy-start.5 = (bf16[128,8]{0,1:T(8,128)(2,1)S(1)}, bf16[128,8]{0,1:T(8,128)(2,1)}, u32[]{:S(2)}) copy-start(bf16[128,8]{0,1:T(8,128)(2,1)} %param.14) | copy-start | bytes 6148
  20.0 22.9 %copy-start.6 = (s32[32]{0:T(128)S(1)}, s32[32]{0:T(128)}, u32[]{:S(2)}) copy-start(s32[32]{0:T(128)} %param.11) | copy-start | bytes 388
  43.9 9.8 %all-to-all-start.1 = ((bf16[8,32,4]{1,2,0:T(4,128)(2,1)}), bf16[8,32,4]{1,2,0:T(4,128)(2,1)S(1)}, u32[]{:S(2)}, u32[]{:S(2)}) async-start(bf16[8,32,4]{1,2,0:T(4,128)(2,1)} %broadcast_in_dim.4), calls=%async_computation.1 | async-start | bytes 16384 | tf_op jit(solution)/shard_map/all_to_all | solution.py:84
  53.8 14.7 %all-to-all-start = ((bf16[256,4,96]{2,1,0:T(4,128)(2,1)}), bf16[256,4,96]{2,1,0:T(4,128)(2,1)S(1)}, u32[]{:S(2)}, u32[]{:S(2)}) async-start(bf16[256,4,96]{2,1,0:T(4,128)(2,1)} %reshape.226), calls=%async_computation | async-start | bytes 524288 | tf_op jit(solution)/shard_map/all_to_all | solution.py:83
  75.9 10.9 %copy-start.1 = (bf16[32,4,256]{2,1,0:T(4,128)(2,1)S(1)}, bf16[32,4,256]{2,1,0:T(4,128)(2,1)}, u32[]{:S(2)}) copy-start(bf16[32,4,256]{2,1,0:T(4,128)(2,1)} %param.9) | copy-start | bytes 196612
  75.9 10.9 %copy-start.3 = (bf16[256,256]{1,0:T(8,128)(2,1)S(1)}, bf16[256,256]{1,0:T(8,128)(2,1)}, u32[]{:S(2)}) copy-start(bf16[256,256]{1,0:T(8,128)(2,1)} %param.15) | copy-start | bytes 393220
  75.9 11.4 %copy-start.4 = (bf16[256,64]{0,1:T(8,128)(2,1)S(1)}, bf16[256,64]{0,1:T(8,128)(2,1)}, u32[]{:S(2)}) copy-start(bf16[256,64]{0,1:T(8,128)(2,1)} %param.16) | copy-start | bytes 98308
  77.0 9.2 %all-to-all-start.2 = ((bf16[8,2,2048]{2,1,0:T(2,128)(2,1)}), bf16[8,2,2048]{2,1,0:T(2,128)(2,1)S(1)}, u32[]{:S(2)}, u32[]{:S(2)}) async-start(bf16[8,2,2048]{2,1,0:T(2,128)(2,1)} %reshape.228), calls=%async_computation.2 | async-start | bytes 131072 | tf_op jit(solution)/shard_map/all_to_all | solution.py:119
  102.7 8.6 %all-to-all-start.3 = ((bf16[2,2,8192]{2,1,0:T(2,128)(2,1)}), bf16[2,2,8192]{2,1,0:T(2,128)(2,1)S(1)}, u32[]{:S(2)}, u32[]{:S(2)}) async-start(bf16[2,2,8192]{2,1,0:T(2,128)(2,1)} %reshape.230), calls=%async_computation.3 | async-start | bytes 131072 | tf_op jit(solution)/shard_map/all_to_all | solution.py:151
